TPU v7x, 512 devices: a 8x2x16 block of a 8x8x16 slice. The times are simulated.
512 devices in a mesh: members: 2 (over y), band: 32 (over z, core), head: 8 (over x).
Axes of the slice: x: 8, y: 2, z: 16, core: 2. Of those that a mesh axis runs over, the one named last changes fastest.
The devices are a block of a 8x8x16 slice.
Arguments:
- grid_feats: bfloat16 [32768, 1024], P(('members', 'band')), parts along dimension 0, may hold values from -6 to 6
- mesh_feats: bfloat16 [32768, 1024], P(('members', 'band')), parts along dimension 0, may hold values from -6 to 6
- enc_in: bfloat16 [3, 1024, 1024], P(None, 'band', 'head'), may hold values from -0.19921875 to 0.19921875
- enc_out: bfloat16 [1024, 1024], P('head', 'band'), may hold values from -0.1875 to 0.1875
- proc_in: bfloat16 [3, 1024, 1024], P(None, 'band', 'head'), may hold values from -0.19921875 to 0.19921875
- proc_out: bfloat16 [1024, 1024], P('head', 'band'), may hold values from -0.1875 to 0.1875
- ff_up: bfloat16 [1024, 4096], P('band', 'head'), may hold values from -0.1875 to 0.1875
- ff_down: bfloat16 [4096, 1024], P('head', 'band'), may hold values from -0.09375 to 0.09375
- dec_in: bfloat16 [3, 1024, 1024], P(None, 'band', 'head'), may hold values from -0.19921875 to 0.19921875
- dec_out: bfloat16 [1024, 1024], P('head', 'band'), may hold values from -0.1875 to 0.1875
- enc_list: int32 [128, 8], replicated, may hold values from 0 to 127, as said below
- enc_count: int32 [128], replicated, may hold values from 1 to 8
- dec_list: int32 [128, 8], replicated, may hold values from 0 to 127, as said below
- dec_count: int32 [128], replicated, may hold values from 1 to 8
- window_ids: int32 [16384], replicated, may hold values from 0 to 20, never falling along the last dimension, each value on 1 to 1536 neighbouring positions
Outputs:
- grid_out: bfloat16 [32768, 1024], P(('members', 'band', 'head')), parts along dimension 0
There are 2 independent parts, one for each index of `members`. A program takes and returns all parts, laid end to end along the dimension named above; an argument that names none is the same for every part. Nothing has to cross between parts.
Inputs may be any that keep to these rules, and one draw needn't show every extreme that they name: `enc_list`: each row holds distinct block numbers. Every block listed for mesh block m lies in the band of 512 grid points with the same band number as m's band of 512 nodes, or in the band just before or just after it. Only the first enc_count[m] slots of row m of enc_list are used. `dec_list`: each row holds distinct block numbers. Every block listed for grid block g lies in the band of 512 mesh nodes with the same band number as g's band of 512 grid points, or in the band just before or just after it. Only the first dec_count[g] slots of row g of dec_list are used. `window_ids`: never falls along the nodes; each window holds at most 1536 consecutive nodes.
All inputs are finite; a program needn't handle non-finite values.
Results may differ from a plain program's by a relative error of at most 0.02.
Values may be sent and summed in bfloat16 or wider, within the bound.
A program may use at most 64 MiB of HBM per device.

v0:
```python
import jax
import jax.numpy as jnp
from jax import lax
from jax.sharding import Mesh
from jax.sharding import PartitionSpec as P

HD = 64
BLOCK = 128
WINDOW = 1536
BAND = ("band_0", "band_1")
MEMBERS_BAND = ("members", "band_0", "band_1")
MEMBERS_BAND_HEAD = ("members", "band_0", "band_1", "head")
EPSILON = 1e-05
NEGATIVE = -1e30


def joined_along(blocks, dim):
    dims = list(blocks.shape[1:])
    dims[dim] *= blocks.shape[0]
    return jnp.moveaxis(blocks, 0, dim).reshape(dims)


def all_blocks(array, axes, order):
    blocks = array[None]
    for k in order:
        blocks = lax.all_gather(blocks, axes[k], axis=0, tiled=True)
    block = [lax.axis_size(axes[k]) for k in reversed(order)]
    blocks = blocks.reshape(*block, *array.shape)
    turned = sorted(range(len(order)), key=lambda place: order[len(order) - 1 - place])
    return blocks.transpose(*turned, *range(len(order), blocks.ndim)).reshape(-1, *array.shape)


def whole_of(array, axes, order, dim):
    return joined_along(all_blocks(array, axes, order), dim)


def padded(block, sides, width):
    for axis, dim in sides:
        count = lax.axis_size(axis)
        forward = [(i, i + 1) for i in range(count - 1)]
        backward = [(target, source) for source, target in forward]
        low = lax.ppermute(
            lax.slice_in_dim(block, block.shape[dim] - width, None, axis=dim), axis, forward
        )
        high = lax.ppermute(lax.slice_in_dim(block, 0, width, axis=dim), axis, backward)
        block = jnp.concatenate([low, block, high], axis=dim)
    return block


def copy_for_each(array, axis):
    size = lax.axis_size(axis)
    return lax.all_to_all(
        jnp.broadcast_to(array[None], (size, *array.shape)), axis, 0, 0, tiled=True
    )


def gathered_copies(array, axis, dim):
    return joined_along(copy_for_each(array, axis), dim)


def shifted(block, axis, distance):
    devices = range(lax.axis_size(axis))
    route = [(i - distance, i) for i in devices if i - distance in devices]
    return lax.ppermute(block, axis, route)


def split_up(array, dim, size):
    dims = array.shape
    blocks = array.reshape(*dims[:dim], size, dims[dim] // size, *dims[dim + 1 :])
    return jnp.moveaxis(blocks, dim, 0)


def summed_on_arrival(array, axis, dim):
    size = lax.axis_size(axis)
    blocks = lax.all_to_all(split_up(array, dim, size), axis, 0, 0, tiled=True)
    return jnp.sum(blocks.astype(jnp.float32), axis=0)


def normed(source):
    values_f = source.astype(jnp.float32)
    centred = values_f - jnp.mean(values_f, axis=-1, keepdims=True)
    variance = jnp.mean(centred * centred, axis=-1, keepdims=True)
    return (centred * lax.rsqrt(variance + EPSILON)).astype(jnp.bfloat16)


def fold_three(sources, carry, piece):
    width = piece.shape[1]
    return tuple(
        (
            total
            + jnp.dot(
                lax.slice_in_dim(source, 0, width, axis=1),
                piece[which],
                preferred_element_type=jnp.float32,
            )
            for which, (total, source) in enumerate(zip(carry, sources))
        )
    )


def fold_rows(source, total, piece):
    return total + jnp.dot(
        lax.slice_in_dim(source, 0, piece.shape[0], axis=1),
        piece,
        preferred_element_type=jnp.float32,
    )


def columns_of(source, piece):
    return jnp.dot(source, piece, preferred_element_type=jnp.float32)


def head_scores(queries, key_rows, head_index, allowed):
    lower = head_index * HD
    scores = jnp.einsum(
        "qd,kd->qk",
        queries[:, lower : lower + HD],
        key_rows[:, lower : lower + HD],
        preferred_element_type=jnp.float32,
    ) * HD ** (-0.5)
    scores = jnp.where(allowed, scores, NEGATIVE)
    maxima = jnp.max(scores, axis=1, keepdims=True)
    expo = jnp.where(allowed, jnp.exp(scores - maxima), 0.0)
    return (expo, maxima, jnp.sum(expo, axis=1, keepdims=True))


def attend_rounded(queries, key_rows, value_rows, allowed):
    outputs = []
    for head_index in range(queries.shape[1] // HD):
        expo, maxima, totals = head_scores(queries, key_rows, head_index, allowed)
        weights = (expo / totals).astype(jnp.bfloat16)
        lower = head_index * HD
        outputs.append(
            jnp.dot(weights, value_rows[:, lower : lower + HD], preferred_element_type=jnp.float32)
        )
    return jnp.concatenate(outputs, axis=1).astype(jnp.bfloat16)


def partial_attend(queries, key_rows, value_rows, allowed):
    outputs, maxima_all, totals_all = ([], [], [])
    for head_index in range(queries.shape[1] // HD):
        expo, maxima, totals = head_scores(queries, key_rows, head_index, allowed)
        lower = head_index * HD
        outputs.append(jnp.dot(expo, value_rows[:, lower : lower + HD].astype(jnp.float32)))
        maxima_all.append(maxima)
        totals_all.append(totals)
    return (
        jnp.concatenate(outputs, axis=1),
        jnp.concatenate(maxima_all, axis=1),
        jnp.concatenate(totals_all, axis=1),
    )


def listed_attend(queries, key_pool, value_pool, lists, counts, base_block, rounded):
    width = queries.shape[1]
    rows = queries.shape[0]
    pool_blocks = key_pool.shape[0] // BLOCK
    key_blocks = key_pool.reshape(pool_blocks, BLOCK, width)
    value_blocks = value_pool.reshape(pool_blocks, BLOCK, width)
    slots = lists.shape[1]

    def one_block(index):
        listed = lists[index] - base_block
        inside = (
            (listed >= 0)
            & (listed < pool_blocks)
            & (jnp.arange(slots, dtype=jnp.int32) < counts[index])
        )
        safe = jnp.clip(listed, 0, pool_blocks - 1)
        block_keys = key_blocks[safe].reshape(slots * BLOCK, width)
        block_values = value_blocks[safe].reshape(slots * BLOCK, width)
        allowed = jnp.repeat(inside, BLOCK)[None, :]
        block_queries = lax.dynamic_slice_in_dim(queries, index * BLOCK, BLOCK, 0)
        if rounded:
            return attend_rounded(block_queries, block_keys, block_values, allowed)
        return partial_attend(block_queries, block_keys, block_values, allowed)

    result = lax.map(one_block, jnp.arange(rows // BLOCK, dtype=jnp.int32))
    return jax.tree.map(lambda stacked: stacked.reshape(rows, stacked.shape[-1]), result)


def normalize(outputs, totals):
    rows = outputs.shape[0]
    heads_here = totals.shape[1]
    shaped = outputs.reshape(rows, heads_here, HD) / totals[:, :, None]
    return shaped.reshape(rows, heads_here * HD).astype(jnp.bfloat16)


def per_device(
    grid_feats,
    mesh_feats,
    enc_in,
    enc_out,
    proc_in,
    proc_out,
    ff_up,
    ff_down,
    dec_in,
    dec_out,
    enc_list,
    enc_count,
    dec_list,
    dec_count,
    window_ids,
):
    band_index = lax.axis_index(BAND)
    grid_rows = grid_feats.shape[0]
    mesh_rows = mesh_feats.shape[0]
    width = enc_in.shape[2]
    grid_blocks = grid_rows // BLOCK
    mesh_blocks = mesh_rows // BLOCK
    grid_norm = normed(grid_feats)
    mesh_norm = normed(mesh_feats)
    grid_zeros = jnp.zeros((grid_rows, width), jnp.float32)
    mesh_zeros = jnp.zeros((mesh_rows, width), jnp.float32)
    enc_q, enc_k, enc_v = fold_three(
        (mesh_norm, grid_norm, grid_norm),
        (mesh_zeros, grid_zeros, grid_zeros),
        whole_of(enc_in, BAND, (0, 1), 1),
    )
    enc_q = enc_q.astype(jnp.bfloat16)
    enc_k = enc_k.astype(jnp.bfloat16)
    enc_v = enc_v.astype(jnp.bfloat16)
    my_lists = lax.dynamic_slice_in_dim(enc_list, band_index * mesh_blocks, mesh_blocks, 0)
    my_counts = lax.dynamic_slice_in_dim(enc_count, band_index * mesh_blocks, mesh_blocks, 0)
    pool = padded(jnp.stack([enc_k, enc_v]), ((BAND, 1),), grid_rows)
    outputs, maxima, totals = listed_attend(
        enc_q, pool[0], pool[1], my_lists, my_counts, (band_index - 1) * grid_blocks, False
    )
    enc_attn = normalize(outputs, totals)
    enc_terms = columns_of(enc_attn, gathered_copies(enc_out, BAND, 1))
    mesh_state = mesh_feats.astype(jnp.float32) + lax.psum(
        enc_terms.astype(jnp.bfloat16), "head"
    ).astype(jnp.float32)
    proc_norm = normed(mesh_state)
    proc_q, proc_k, proc_v = fold_three(
        (proc_norm, proc_norm, proc_norm),
        (mesh_zeros, mesh_zeros, mesh_zeros),
        whole_of(proc_in, BAND, (0, 1), 1),
    )
    proc_q = proc_q.astype(jnp.bfloat16)
    pairs = jnp.stack([proc_k.astype(jnp.bfloat16), proc_v.astype(jnp.bfloat16)])
    reach = (WINDOW + mesh_rows - 2) // mesh_rows
    slab_parts = {0: pairs}
    for distance in range(1, reach + 1):
        for direction in (1, -1):
            slab_parts[direction * distance] = shifted(pairs, BAND, -direction * distance)
    slab = jnp.concatenate([slab_parts[offset] for offset in range(-reach, reach + 1)], axis=1)
    padded_ids = jnp.pad(window_ids, (reach * mesh_rows, reach * mesh_rows), constant_values=-1)
    slab_ids = lax.dynamic_slice_in_dim(
        padded_ids, band_index * mesh_rows, (2 * reach + 1) * mesh_rows, 0
    )
    slab_start = (band_index - reach) * mesh_rows
    span = 2 * WINDOW

    def window_block(index):
        first = band_index * mesh_rows + index * BLOCK
        first_id = window_ids[first]
        window_start = jnp.sum((window_ids < first_id).astype(jnp.int32))
        local = window_start - slab_start
        block_keys = lax.dynamic_slice_in_dim(slab[0], local, span, 0)
        block_values = lax.dynamic_slice_in_dim(slab[1], local, span, 0)
        key_ids = lax.dynamic_slice_in_dim(slab_ids, local, span, 0)
        query_ids = lax.dynamic_slice_in_dim(window_ids, first, BLOCK, 0)
        block_queries = lax.dynamic_slice_in_dim(proc_q, index * BLOCK, BLOCK, 0)
        return attend_rounded(
            block_queries, block_keys, block_values, query_ids[:, None] == key_ids[None, :]
        )

    proc_attn = lax.map(window_block, jnp.arange(mesh_blocks, dtype=jnp.int32)).reshape(
        mesh_rows, width
    )
    proc_terms = columns_of(proc_attn, gathered_copies(proc_out, BAND, 1))
    mesh_mid = mesh_state + lax.psum(proc_terms.astype(jnp.bfloat16), "head").astype(jnp.float32)
    ff_norm = normed(mesh_mid)
    hidden = fold_rows(
        ff_norm,
        jnp.zeros((mesh_rows, ff_up.shape[1]), jnp.float32),
        whole_of(ff_up, BAND, (0, 1), 0),
    )
    hidden = jax.nn.gelu(hidden, approximate=False).astype(jnp.bfloat16)
    ff_terms = columns_of(hidden, whole_of(ff_down, BAND, (0, 1), 1))
    mesh_final = mesh_mid + lax.psum(ff_terms.astype(jnp.bfloat16), "head").astype(jnp.float32)
    final_norm = normed(mesh_final)
    dec_q, dec_k, dec_v = fold_three(
        (grid_norm, final_norm, final_norm),
        (grid_zeros, mesh_zeros, mesh_zeros),
        whole_of(dec_in, BAND, (0, 1), 1),
    )
    dec_q = dec_q.astype(jnp.bfloat16)
    dec_pool = padded(
        jnp.stack([dec_k.astype(jnp.bfloat16), dec_v.astype(jnp.bfloat16)]), ((BAND, 1),), mesh_rows
    )
    grid_lists = lax.dynamic_slice_in_dim(dec_list, band_index * grid_blocks, grid_blocks, 0)
    grid_counts = lax.dynamic_slice_in_dim(dec_count, band_index * grid_blocks, grid_blocks, 0)
    dec_attn = listed_attend(
        dec_q,
        dec_pool[0],
        dec_pool[1],
        grid_lists,
        grid_counts,
        (band_index - 1) * mesh_blocks,
        True,
    )
    full_out = gathered_copies(dec_out, BAND, 1)
    share = grid_rows // lax.axis_size("head")
    summed = summed_on_arrival(
        jnp.dot(
            lax.slice_in_dim(dec_attn, 0, share * lax.axis_size("head"), axis=0),
            full_out,
            preferred_element_type=jnp.float32,
        ).astype(jnp.bfloat16),
        "head",
        0,
    )
    residual = lax.dynamic_slice_in_dim(
        grid_feats, lax.axis_index("head") * share, share, 0
    ).astype(jnp.float32)
    return (residual + summed).astype(jnp.bfloat16)


def solution(mesh):
    finer = Mesh(
        mesh.devices.reshape(mesh.shape["members"], 16, 2, mesh.shape["head"]),
        ("members", "band_0", "band_1", "head"),
    )
    placed = (
        P(MEMBERS_BAND, None),
        P(MEMBERS_BAND, None),
        P(None, BAND, "head"),
        P("head", BAND),
        P(None, BAND, "head"),
        P("head", BAND),
        P(BAND, "head"),
        P("head", BAND),
        P(None, BAND, "head"),
        P("head", BAND),
        P(),
        P(),
        P(),
        P(),
        P(),
    )
    return jax.shard_map(
        per_device,
        mesh=finer,
        in_specs=placed,
        out_specs=P(MEMBERS_BAND_HEAD, None),
        check_vma=False,
    )
```

profile of v0, /device:TPU:65, one launch (start us, length us, event | category | flops | bytes accessed | tf_op | source)
XLA Modules:
  0.0 632.4 jit_solution(11155338328643831637)
XLA Ops:
  7.4 1.5 convert_reduce_fusion.2
  8.9 1.6 fusion.64
  10.9 64.3 %all-gather.1 = bf16[48,32,128]{2,1,0:T(8,128)(2,1)S(1)} all-gather(bf16[3,32,128]{2,1,0:T(8,128)(2,1)S(1)} %copy-done.15), channel_id=3, replica_groups=mesh['members'=2,'band_0'=16,'band_1'=2,'head'=8] {'band_0'}, dimensions={0}, use_global_device_ids=true | all-gather | bytes 417792 | tf_op jit(solution)/shard_map/all_gather | solution.py:26
  75.2 9.4 %all_gather.33 = bf16[32,3,32,128]{3,2,1,0:T(8,128)(2,1)S(1)} all-gather(bf16[16,3,32,128]{3,2,1,0:T(8,128)(2,1)S(1)} %bitcast.225), channel_id=1, replica_groups=mesh['members'=2,'band_0'=16,'band_1'=2,'head'=8] {'band_1'}, dimensions={0}, use_global_device_ids=true | all-gather | bytes 1179648 | tf_op jit(solution)/shard_map/all_gather | solution.py:26
  85.8 2.3 collective-permute-start.1
  88.1 3.3 collective-permute-start
  92.2 4.8 all-to-all-start
  100.3 39.7 %while.34 = (s32[]{:T(128)}, f32[4,128,128]{2,1,0:T(8,128)}, f32[4,128,2]{1,2,0:T(2,128)}, s32[4]{0:T(128)}, s32[4,8]{1,0:T(4,128)S(1)}, /*index=5*/s32[]{:T(128...) while((s32[]{:T(128)}, f32[4,128,128]{2,1,0:T(8,128)}, ...), condition=%wide.region_9.10_spmd, body=%wide.region_4.9_spmd.sunk | while | flops 69223264 | bytes 5784073 | solution.py:178
  104.6 1.2 dynamic_slice.120
  114.5 1.2 dynamic_slice.120
  120.2 1.2 dynamic_slice.119
  124.5 1.2 dynamic_slice.120
  134.4 1.2 dynamic_slice.120
  142.0 2.4 convolution_convert_fusion.6
  144.5 24.8 %all-gather.4 = bf16[8192,32]{0,1:T(8,128)(2,1)S(1)} all-gather(bf16[512,32]{0,1:T(8,128)(2,1)S(1)} %copy-done.13), channel_id=6, replica_groups=mesh['members'=2,'band_0'=16,'band_1'=2,'head'=8] {'band_0'}, dimensions={0}, use_global_device_ids=true | all-gather | bytes 557056 | tf_op jit(solution)/shard_map/all_gather | solution.py:26
  171.1 16.2 %all-to-all-start.1 = ((bf16[32,128,32]{1,2,0:T(8,128)(2,1)}), bf16[32,128,32]{1,2,0:T(8,128)(2,1)S(1)}, u32[]{:S(2)}, u32[]{:S(2)}) async-start(bf16[32,128,32]{1,2,0:T(8,128)(2,1)} %broadcast_in_dim.159), calls=%async_computation.1 | async-start | bytes 524288 | tf_op jit(solution)/shard_map/all_to_all | solution.py:52
  187.4 37.6 %all-gather.3 = bf16[512,512]{1,0:T(8,128)(2,1)} all-gather(bf16[32,512]{1,0:T(8,128)(2,1)S(1)} %copy-done.14), channel_id=5, replica_groups=mesh['members'=2,'band_0'=16,'band_1'=2,'head'=8] {'band_0'}, dimensions={0}, use_global_device_ids=true | all-gather | bytes 557056 | tf_op jit(solution)/shard_map/all_gather | solution.py:26
  225.1 23.3 %all-gather.2 = bf16[48,32,128]{2,1,0:T(8,128)(2,1)S(1)} all-gather(bf16[3,32,128]{2,1,0:T(8,128)(2,1)S(1)} %copy-done.16), channel_id=4, replica_groups=mesh['members'=2,'band_0'=16,'band_1'=2,'head'=8] {'band_0'}, dimensions={0}, use_global_device_ids=true | all-gather | bytes 417792 | tf_op jit(solution)/shard_map/all_gather | solution.py:26
  248.4 13.6 %all_gather.35 = bf16[32,3,32,128]{3,2,1,0:T(8,128)(2,1)S(1)} all-gather(bf16[16,3,32,128]{3,2,1,0:T(8,128)(2,1)S(1)} %bitcast.226), channel_id=1, replica_groups=mesh['members'=2,'band_0'=16,'band_1'=2,'head'=8] {'band_1'}, dimensions={0}, use_global_device_ids=true | all-gather | bytes 1179648 | tf_op jit(solution)/shard_map/all_gather | solution.py:26
  262.2 1.7 fusion.66
  265.8 4.0 collective-permute-start.2
  269.9 3.3 collective-permute-start.3
  273.2 2.5 collective-permute-start.4
  275.7 2.0 collective-permute-start.5
  277.7 1.3 collective-permute-start.6
  279.4 1.3 collective-permute-start.7
  281.8 1.9 collective-permute-done.4
  284.9 3.0 collective-permute-done.6
  288.0 10.1 %collective-permute-done.7 = bf16[2,512,128]{2,1,0:T(8,128)(2,1)S(1)} collective-permute-done((bf16[2,512,128]{2,1,0:T(8,128)(2,1)S(1)}, bf16[2,512,128]{2,1,0:T(8,128)(2,1)S(1)}, u32[]{:S(2)}, u32[]{:S(2)}) %collective-permute-start.7) | collective-permute-done | bytes 262176 | tf_op jit(solution)/shard_map/ppermute | solution.py:64
  299.4 49.0 %while.35 = (s32[]{:T(128)}, bf16[4,128,128]{2,1,0:T(8,128)(2,1)S(1)}, s32[4]{0:T(128)S(1)}, s32[]{:T(128)}, s32[16384]{0:T(1024)S(1)}, /*index=5*/s32[]{:T(128)...) while((s32[]{:T(128)}, ...), condition=%wide.region_19.20_spmd, body=%wide.region_13.19_spmd.sunk | while | flops 211287568 | bytes 26145704 | solution.py:270
  299.4 1.6 fusion.224
  302.8 1.3 convert_reduce_fusion.5
  304.7 1.6 dynamic-slice_bitcast_fusion.3
  306.5 1.8 fusion.225
  311.6 1.6 fusion.224
  315.1 1.3 convert_reduce_fusion.5
  317.0 1.6 dynamic-slice_bitcast_fusion.3
  318.7 1.8 fusion.225
  323.9 1.6 fusion.224
  327.3 1.3 convert_reduce_fusion.5
  329.3 1.6 dynamic-slice_bitcast_fusion.3
  331.0 1.8 fusion.225
  336.1 1.6 fusion.224
  339.6 1.3 convert_reduce_fusion.5
  341.5 1.6 dynamic-slice_bitcast_fusion.3
  343.3 1.8 fusion.225
  348.4 1.4 convolution_convert_fusion.5
  350.2 2.8 copy.72
  353.0 2.3 copy.70
  355.3 77.1 %all-reduce.7.cloned.1.call-done = bf16[512,1024]{1,0:T(8,128)(2,1)} async-done(((bf16[512,1024]{1,0:T(8,128)(2,1)}), bf16[512,1024]{1,0:T(8,128)(2,1)}) %all-reduce.7.cloned.1.call-update) | async-done | bytes 1048592 | tf_op jit(solution)/shard_map/psum | solution.py:274
  432.5 2.0 fusion.150
  435.7 5.6 convolution_convert_fusion.7
  441.4 26.9 %all-gather = bf16[48,32,128]{2,1,0:T(8,128)(2,1)S(1)} all-gather(bf16[3,32,128]{2,1,0:T(8,128)(2,1)S(1)} %copy-done.17), channel_id=2, replica_groups=mesh['members'=2,'band_0'=16,'band_1'=2,'head'=8] {'band_0'}, dimensions={0}, use_global_device_ids=true | all-gather | bytes 417792 | tf_op jit(solution)/shard_map/all_gather | solution.py:26
  468.3 14.2 %all_gather.31 = bf16[32,3,32,128]{3,2,1,0:T(8,128)(2,1)S(1)} all-gather(bf16[16,3,32,128]{3,2,1,0:T(8,128)(2,1)S(1)} %bitcast.227), channel_id=1, replica_groups=mesh['members'=2,'band_0'=16,'band_1'=2,'head'=8] {'band_1'}, dimensions={0}, use_global_device_ids=true | all-gather | bytes 1179648 | tf_op jit(solution)/shard_map/all_gather | solution.py:26
  483.4 45.9 %all-reduce.9.cloned.1.call-done = bf16[512,1024]{1,0:T(8,128)(2,1)} async-done(((bf16[512,1024]{1,0:T(8,128)(2,1)}), bf16[512,1024]{1,0:T(8,128)(2,1)}) %all-reduce.9.cloned.1.call-update) | async-done | bytes 1048592 | tf_op jit(solution)/shard_map/psum | solution.py:283
  529.3 1.6 fusion.89
  533.3 7.6 %collective-permute-start.9 = (bf16[2,512,128]{2,1,0:T(8,128)(2,1)S(1)}, bf16[2,512,128]{2,1,0:T(8,128)(2,1)S(1)}, u32[]{:S(2)}, u32[]{:S(2)}) collective-permute-start(bf16[2,512,128]{2,1,0:T(8,128)(2,1)S(1)} %pad_maximum_fusion.6), channel_id=1, source_target_pairs={{8,0},{16,8},{24,16},{32,24},{40,32},{48,40},{56,48},{64,56},{72,6... | collective-permute-start | bytes 786440 | tf_op jit(solution)/shard_map/ppermute | solution.py:45
  540.9 3.2 collective-permute-start.8
  544.8 12.4 %all-to-all-start.2 = ((bf16[32,128,32]{1,2,0:T(8,128)(2,1)}), bf16[32,128,32]{1,2,0:T(8,128)(2,1)S(1)}, u32[]{:S(2)}, u32[]{:S(2)}) async-start(bf16[32,128,32]{1,2,0:T(8,128)(2,1)} %broadcast_in_dim.162), calls=%async_computation.2 | async-start | bytes 524288 | tf_op jit(solution)/shard_map/all_to_all | solution.py:52
  558.0 30.9 %while.36 = (s32[]{:T(128)}, bf16[4,128,128]{2,1,0:T(8,128)(2,1)S(1)}, s32[4]{0:T(128)S(1)}, s32[4,8]{1,0:T(4,128)S(1)}, s32[]{:T(128)}, /*index=5*/s32[4]{0:T(1...) while((s32[]{:T(128)}, ...), condition=%wide.region_31.32_spmd, body=%wide.region_26.31_spmd.sunk | while | flops 69812832 | bytes 5553661 | solution.py:178
  588.9 1.4 convolution_convert_fusion.4
  590.4 3.9 all-to-all-start.3
  594.3 29.2 %all-to-all-done.3 = bf16[8,64,1024]{2,1,0:T(8,128)(2,1)S(1)} async-done(((bf16[8,64,1024]{2,1,0:T(8,128)(2,1)}), bf16[8,64,1024]{2,1,0:T(8,128)(2,1)S(1)}, u32[]{:S(2)}, u32[]{:S(2)}) %all-to-all-start.3) | async-done | bytes 1048608 | tf_op jit(solution)/shard_map/all_to_all | solution.py:75
  623.7 1.6 add_convert_fusion
  (327 shorter events, 84.2 us)
Async XLA Ops:
  7.4 3.2 copy-start.7
  8.9 2.0 copy-start.15
  10.9 74.3 %copy-start.5 = (bf16[512,1024]{1,0:T(8,128)(2,1)}, bf16[512,1024]{1,0:T(8,128)(2,1)S(1)}, u32[]{:S(2)}) copy-start(bf16[512,1024]{1,0:T(8,128)(2,1)S(1)} %fusion.65) | copy-start | bytes 3145732
  84.8 6.6 %copy-start.19 = (bf16[128,32]{0,1:T(8,128)(2,1)S(1)}, bf16[128,32]{0,1:T(8,128)(2,1)}, u32[]{:S(2)}) copy-start(bf16[128,32]{0,1:T(8,128)(2,1)} %param.24) | copy-start | bytes 24580
  84.8 12.3 %copy-start.1 = (bf16[512,1024]{1,0:T(8,128)(2,1)S(1)}, bf16[512,1024]{1,0:T(8,128)(2,1)}, u32[]{:S(2)}) copy-start(bf16[512,1024]{1,0:T(8,128)(2,1)} %param.22) | copy-start | bytes 3145732
  85.7 12.0 %copy-start.22 = (s32[128,8]{0,1:T(8,128)S(1)}, s32[128,8]{0,1:T(8,128)}, u32[]{:S(2)}) copy-start(s32[128,8]{0,1:T(8,128)} %param.31) | copy-start | bytes 12292
  85.7 12.0 %copy-start.23 = (s32[128,8]{0,1:T(8,128)S(1)}, s32[128,8]{0,1:T(8,128)}, u32[]{:S(2)}) copy-start(s32[128,8]{0,1:T(8,128)} %param.33) | copy-start | bytes 12292
  85.7 12.8 %copy-start.24 = (s32[128]{0:T(128)S(1)}, s32[128]{0:T(128)}, u32[]{:S(2)}) copy-start(s32[128]{0:T(128)} %param.32) | copy-start | bytes 1540
  85.8 13.8 %collective-permute-start.1 = (bf16[2,512,128]{2,1,0:T(8,128)(2,1)S(1)}, bf16[2,512,128]{2,1,0:T(8,128)(2,1)S(1)}, u32[]{:S(2)}, u32[]{:S(2)}) collective-permute-start(bf16[2,512,128]{2,1,0:T(8,128)(2,1)S(1)} %pad_maximum_fusion.4), channel_id=1, source_target_pairs={{8,0},{16,8},{24,16},{32,24},{40,32},{48,40},{56,48},{64,56},{72,6... | collective-permute-start | bytes 786440 | tf_op jit(solution)/shard_map/ppermute | solution.py:45
  88.1 11.5 %collective-permute-start = (bf16[2,512,128]{2,1,0:T(8,128)(2,1)S(1)}, bf16[2,512,128]{2,1,0:T(8,128)(2,1)S(1)}, u32[]{:S(2)}, u32[]{:S(2)}) collective-permute-start(bf16[2,512,128]{2,1,0:T(8,128)(2,1)S(1)} %pad_maximum_fusion.4), channel_id=1, source_target_pairs={{0,8},{8,16},{16,24},{24,32},{32,40},{40,48},{48,56},{56,64},{64,7... | collective-permute-start | bytes 786440 | tf_op jit(solution)/shard_map/ppermute | solution.py:42
  92.2 49.8 %all-to-all-start = ((bf16[32,128,32]{1,2,0:T(8,128)(2,1)}), bf16[32,128,32]{1,2,0:T(8,128)(2,1)}, u32[]{:S(2)}, u32[]{:S(2)}) async-start(bf16[32,128,32]{1,2,0:T(8,128)(2,1)} %broadcast_in_dim.157), calls=%async_computation | async-start | bytes 524288 | tf_op jit(solution)/shard_map/all_to_all | solution.py:52
  97.0 165.2 %all-reduce.5.cloned.1.call-start = ((), (), s32[]{:S(2)}) async-start(), calls=%async_computation.4 | async-start | bytes 2097152 | tf_op jit(solution)/shard_map/psum | solution.py:232
  140.8 3.7 copy-start.13
  144.3 26.0 %copy-start.20 = (bf16[128,32]{0,1:T(8,128)(2,1)S(1)}, bf16[128,32]{0,1:T(8,128)(2,1)}, u32[]{:S(2)}) copy-start(bf16[128,32]{0,1:T(8,128)(2,1)} %param.26) | copy-start | bytes 24580
  144.3 43.0 %copy-start.14 = (bf16[32,512]{1,0:T(8,128)(2,1)S(1)}, bf16[32,512]{1,0:T(8,128)(2,1)}, u32[]{:S(2)}) copy-start(bf16[32,512]{1,0:T(8,128)(2,1)} %param.27) | copy-start | bytes 98308
  144.4 205.8 %all-gather.10.cloned.1.call-start = ((), (), s32[]{:S(2)}) async-start(), calls=%async_computation.7 | async-start | bytes 1572864 | tf_op jit(solution)/shard_map/all_gather | solution.py:26
  169.3 55.8 %copy-start.16 = (bf16[3,32,128]{2,1,0:T(8,128)(2,1)S(1)}, bf16[3,32,128]{2,1,0:T(8,128)(2,1)}, u32[]{:S(2)}) copy-start(bf16[3,32,128]{2,1,0:T(8,128)(2,1)} %param.25) | copy-start | bytes 73732
  171.1 177.3 %all-to-all-start.1 = ((bf16[32,128,32]{1,2,0:T(8,128)(2,1)}), bf16[32,128,32]{1,2,0:T(8,128)(2,1)S(1)}, u32[]{:S(2)}, u32[]{:S(2)}) async-start(bf16[32,128,32]{1,2,0:T(8,128)(2,1)} %broadcast_in_dim.159), calls=%async_computation.1 | async-start | bytes 524288 | tf_op jit(solution)/shard_map/all_to_all | solution.py:52
  187.3 165.7 %all-gather.8.cloned.1.call-start = ((), (), s32[]{:S(2)}) async-start(), calls=%async_computation.6 | async-start | bytes 1572864 | tf_op jit(solution)/shard_map/all_gather | solution.py:26
  225.0 207.4 %all-reduce.7.cloned.1.call-start = ((), (), s32[]{:S(2)}) async-start(), calls=%async_computation.5 | async-start | bytes 2097152 | tf_op jit(solution)/shard_map/psum | solution.py:274
  262.2 1.7 copy-start.4
  264.8 5.0 copy-start.9
  265.8 13.7 %collective-permute-start.2 = (bf16[2,512,128]{2,1,0:T(8,128)(2,1)S(1)}, bf16[2,512,128]{2,1,0:T(8,128)(2,1)}, u32[]{:S(2)}, u32[]{:S(2)}) collective-permute-start(bf16[2,512,128]{2,1,0:T(8,128)(2,1)S(1)} %pad_maximum_fusion.5), channel_id=1, source_target_pairs={{0,24},{8,32},{16,40},{24,48},{32,56},{40,64},{48,72},{56,80},{64,... | collective-permute-start | bytes 786440 | tf_op jit(solution)/shard_map/ppermute | solution.py:64
  269.9 11.8 %collective-permute-start.3 = (bf16[2,512,128]{2,1,0:T(8,128)(2,1)S(1)}, bf16[2,512,128]{2,1,0:T(8,128)(2,1)S(1)}, u32[]{:S(2)}, u32[]{:S(2)}) collective-permute-start(bf16[2,512,128]{2,1,0:T(8,128)(2,1)S(1)} %pad_maximum_fusion.5), channel_id=1, source_target_pairs={{0,16},{8,24},{16,32},{24,40},{32,48},{40,56},{48,64},{56,72},{64,... | collective-permute-start | bytes 786440 | tf_op jit(solution)/shard_map/ppermute | solution.py:64
  273.2 10.5 %collective-permute-start.4 = (bf16[2,512,128]{2,1,0:T(8,128)(2,1)S(1)}, bf16[2,512,128]{2,1,0:T(8,128)(2,1)S(1)}, u32[]{:S(2)}, u32[]{:S(2)}) collective-permute-start(bf16[2,512,128]{2,1,0:T(8,128)(2,1)S(1)} %pad_maximum_fusion.5), channel_id=1, source_target_pairs={{0,8},{8,16},{16,24},{24,32},{32,40},{40,48},{48,56},{56,64},{64,7... | collective-permute-start | bytes 786440 | tf_op jit(solution)/shard_map/ppermute | solution.py:64
  275.7 9.1 %collective-permute-start.5 = (bf16[2,512,128]{2,1,0:T(8,128)(2,1)S(1)}, bf16[2,512,128]{2,1,0:T(8,128)(2,1)S(1)}, u32[]{:S(2)}, u32[]{:S(2)}) collective-permute-start(bf16[2,512,128]{2,1,0:T(8,128)(2,1)S(1)} %pad_maximum_fusion.5), channel_id=1, source_target_pairs={{8,0},{16,8},{24,16},{32,24},{40,32},{48,40},{56,48},{64,56},{72,6... | collective-permute-start | bytes 786440 | tf_op jit(solution)/shard_map/ppermute | solution.py:64
  277.7 10.2 %collective-permute-start.6 = (bf16[2,512,128]{2,1,0:T(8,128)(2,1)S(1)}, bf16[2,512,128]{2,1,0:T(8,128)(2,1)S(1)}, u32[]{:S(2)}, u32[]{:S(2)}) collective-permute-start(bf16[2,512,128]{2,1,0:T(8,128)(2,1)S(1)} %pad_maximum_fusion.5), channel_id=1, source_target_pairs={{16,0},{24,8},{32,16},{40,24},{48,32},{56,40},{64,48},{72,56},{80,... | collective-permute-start | bytes 786440 | tf_op jit(solution)/shard_map/ppermute | solution.py:64
  279.4 18.6 %collective-permute-start.7 = (bf16[2,512,128]{2,1,0:T(8,128)(2,1)S(1)}, bf16[2,512,128]{2,1,0:T(8,128)(2,1)S(1)}, u32[]{:S(2)}, u32[]{:S(2)}) collective-permute-start(bf16[2,512,128]{2,1,0:T(8,128)(2,1)S(1)} %pad_maximum_fusion.5), channel_id=1, source_target_pairs={{24,0},{32,8},{40,16},{48,24},{56,32},{64,40},{72,48},{80,56},{88,... | collective-permute-start | bytes 786440 | tf_op jit(solution)/shard_map/ppermute | solution.py:64
  298.1 1.3 copy-start
  306.3 2.0 copy-start.3
  308.8 1.1 copy-start.2
  318.6 2.0 copy-start.3
  321.0 1.1 copy-start.2
  330.8 2.0 copy-start.3
  333.3 1.1 copy-start.2
  343.1 2.0 copy-start.3
  345.6 1.1 copy-start.2
  349.9 179.4 %all-reduce.9.cloned.1.call-start = ((), (), s32[]{:S(2)}) async-start(), calls=%async_computation.8 | async-start | bytes 2097152 | tf_op jit(solution)/shard_map/psum | solution.py:283
  434.5 1.2 copy-start.10
  435.7 5.7 copy-start.17
  529.3 1.6 copy-start.8
  531.4 1.0 copy-start.12
  531.4 1.4 copy-start.11
  531.7 12.3 %copy-start.21 = (bf16[128,32]{0,1:T(8,128)(2,1)S(1)}, bf16[128,32]{0,1:T(8,128)(2,1)}, u32[]{:S(2)}) copy-start(bf16[128,32]{0,1:T(8,128)(2,1)} %param.30) | copy-start | bytes 24580
  532.3 24.9 %copy-start.18 = (s32[4,8]{0,1:T(8,128)S(1)}, s32[4,8]{0,1:T(8,128)}, u32[]{:S(2)}) copy-start(s32[4,8]{0,1:T(8,128)} %get-tuple-element.308) | copy-start | bytes 388
  532.3 25.0 %copy-start.25 = (s32[128]{0:T(128)S(1)}, s32[128]{0:T(128)}, u32[]{:S(2)}) copy-start(s32[128]{0:T(128)} %param.34) | copy-start | bytes 1540
  532.3 25.1 %copy-start.6 = (bf16[512,1024]{1,0:T(8,128)(2,1)S(1)}, bf16[512,1024]{1,0:T(8,128)(2,1)}, u32[]{:S(2)}) copy-start(bf16[512,1024]{1,0:T(8,128)(2,1)} %copy-done.5) | copy-start | bytes 3145732
  533.3 24.6 %collective-permute-start.9 = (bf16[2,512,128]{2,1,0:T(8,128)(2,1)S(1)}, bf16[2,512,128]{2,1,0:T(8,128)(2,1)S(1)}, u32[]{:S(2)}, u32[]{:S(2)}) collective-permute-start(bf16[2,512,128]{2,1,0:T(8,128)(2,1)S(1)} %pad_maximum_fusion.6), channel_id=1, source_target_pairs={{8,0},{16,8},{24,16},{32,24},{40,32},{48,40},{56,48},{64,56},{72,6... | collective-permute-start | bytes 786440 | tf_op jit(solution)/shard_map/ppermute | solution.py:45
  540.9 17.0 %collective-permute-start.8 = (bf16[2,512,128]{2,1,0:T(8,128)(2,1)S(1)}, bf16[2,512,128]{2,1,0:T(8,128)(2,1)S(1)}, u32[]{:S(2)}, u32[]{:S(2)}) collective-permute-start(bf16[2,512,128]{2,1,0:T(8,128)(2,1)S(1)} %pad_maximum_fusion.6), channel_id=1, source_target_pairs={{0,8},{8,16},{16,24},{24,32},{32,40},{40,48},{48,56},{56,64},{64,7... | collective-permute-start | bytes 786440 | tf_op jit(solution)/shard_map/ppermute | solution.py:42
  544.8 44.1 %all-to-all-start.2 = ((bf16[32,128,32]{1,2,0:T(8,128)(2,1)}), bf16[32,128,32]{1,2,0:T(8,128)(2,1)S(1)}, u32[]{:S(2)}, u32[]{:S(2)}) async-start(bf16[32,128,32]{1,2,0:T(8,128)(2,1)} %broadcast_in_dim.162), calls=%async_computation.2 | async-start | bytes 524288 | tf_op jit(solution)/shard_map/all_to_all | solution.py:52
  590.4 33.1 %all-to-all-start.3 = ((bf16[8,64,1024]{2,1,0:T(8,128)(2,1)}), bf16[8,64,1024]{2,1,0:T(8,128)(2,1)S(1)}, u32[]{:S(2)}, u32[]{:S(2)}) async-start(bf16[8,64,1024]{2,1,0:T(8,128)(2,1)} %bitcast.85), calls=%async_computation.3 | async-start | bytes 2097152 | tf_op jit(solution)/shard_map/all_to_all | solution.py:75
Sparse Core Ops, SparseCore 0:
  144.5 84.8 all-reduce.4
  350.0 82.4 all-reduce.6
  441.5 87.7 all-reduce.8
Sparse Core Ops, SparseCore 1:
  170.4 29.2 all-gather.9
  225.1 29.3 all-gather.7
where the time goes:
time: 635 us; the launch traced here: 632 us
  blocking collectives  214 us (34%)
  waiting for transfers between devices  169 us (27%)
  starting transfers between devices  68.7 us (11%)
  local copies, waits for them, and re-layouts  64.8 us (10%)
  matrix products  41.6 us (7%)
  other arithmetic  33 us (5%)
  loops' own time  26.2 us (4%)
  between operations  15.4 us (2%)
    all_gather x8, blocking collectives, all_blocks(): blocks = lax.all_gather(blocks, axes[k], axis=0, tiled=True)  214 us
    psum x1, waiting for transfers between devices, per_device(): lax.psum(proc_terms.astype(jnp.bfloat16), 'head').astype(jnp.float32)  77.1 us
    psum x1, waiting for transfers between devices, per_device(): lax.psum(ff_terms.astype(jnp.bfloat16), 'head').astype(jnp.float32)  45.9 us
    all_to_all x3, starting transfers between devices, copy_for_each(): lax.all_to_all(jnp.broadcast_to(array[None], (size, *array.shape)), axis,...  33.5 us
    all_to_all x1, waiting for transfers between devices, summed_on_arrival(): blocks = lax.all_to_all(split_up(array, dim, size), axis, 0, 0, tiled=True)  29.2 us
    another operation x2, loops' own time, listed_attend(): result = lax.map(one_block, jnp.arange(rows // BLOCK, dtype=jnp.int32))  20.8 us
    ppermute x6, waiting for transfers between devices, shifted(): return lax.ppermute(block, axis, route)  16.1 us
    dot_general x24, matrix products, head_scores(): jnp.einsum('qd,kd->qk', queries[:, lower:lower + HD], key_rows[:, lower:l...  15 us
  transfers between devices with their start and end apart: 19, of which 7 were waited for; matrix products, arithmetic and copies ran while one was open for 18% of the time, Pallas kernels for 0%

commit v1 on v0

--- a/solution.py
+++ b/solution.py
@@ -23,7 +23,10 @@
 def all_blocks(array, axes, order):
     blocks = array[None]
     for k in order:
-        blocks = lax.all_gather(blocks, axes[k], axis=0, tiled=True)
+        n_dev = lax.axis_size(axes[k])
+        parts = jnp.stack([blocks for _ in range(n_dev)])
+        parts = lax.all_to_all(parts, axes[k], split_axis=0, concat_axis=0)
+        blocks = jnp.concatenate(parts, axis=0)
     block = [lax.axis_size(axes[k]) for k in reversed(order)]
     blocks = blocks.reshape(*block, *array.shape)
     turned = sorted(range(len(order)), key=lambda place: order[len(order) - 1 - place])

time: 635 us -> 664 us (1.046)
  blocking collectives: 214 us -> 25 us
  waiting for transfers between devices: 169 us -> 274 us
  starting transfers between devices: 68.7 us -> 165 us
  local copies, waits for them, and re-layouts: 64.8 us -> 74.5 us
    all_gather x8 -> x0, blocking collectives: 214 us -> none  [all_blocks(): blocks = lax.all_gather(blocks, axes[k], axis=0, tiled=True)]
    all_to_all x0 -> x7, starting transfers between devices: none -> 93.1 us  [all_blocks(): parts = lax.all_to_all(parts, axes[k], split_axis=0, concat_axis=0)]
    psum x1, waiting for transfers between devices: 0.02 us -> 66.1 us  [per_device(): lax.psum(enc_terms.astype(jnp.bfloat16), 'head').astype(jnp.float32)]
    psum x1, waiting for transfers between devices: 45.9 us -> 77.1 us  [per_device(): lax.psum(ff_terms.astype(jnp.bfloat16), 'head').astype(jnp.float32)]
    all_to_all x0 -> x3, blocking collectives: none -> 25 us  [all_blocks(): parts = lax.all_to_all(parts, axes[k], split_axis=0, concat_axis=0)]
    psum x1, waiting for transfers between devices: 77.1 us -> 53.4 us  [per_device(): lax.psum(proc_terms.astype(jnp.bfloat16), 'head').astype(jnp.float32)]
    all_to_all x0 -> x7, waiting for transfers between devices: none -> 16.9 us  [all_blocks(): parts = lax.all_to_all(parts, axes[k], split_axis=0, concat_axis=0)]
    ppermute x2, waiting for transfers between devices: 0.01 us -> 7.83 us  [padded(): lax.ppermute(lax.slice_in_dim(block, 0, width, axis=dim), axis, backward)]
  transfers between devices with their start and end apart: 19 -> 24, of which waited for: 7 -> 12; matrix products, arithmetic and copies ran while one was open for 18% -> 21% of each run, Pallas kernels for 0% -> 0%
where the time goes in v1:
time: 664 us; the launch traced here: 661 us
  waiting for transfers between devices  274 us (41%)
  starting transfers between devices  165 us (25%)
  local copies, waits for them, and re-layouts  74.5 us (11%)
  matrix products  45.4 us (7%)
  other arithmetic  37 us (6%)
  loops' own time  25.3 us (4%)
  blocking collectives  25 us (4%)
  between operations  13.8 us (2%)
    all_to_all x7, starting transfers between devices, all_blocks(): parts = lax.all_to_all(parts, axes[k], split_axis=0, concat_axis=0)  93.1 us
    psum x1, waiting for transfers between devices, per_device(): lax.psum(ff_terms.astype(jnp.bfloat16), 'head').astype(jnp.float32)  77.1 us
    psum x1, waiting for transfers between devices, per_device(): lax.psum(enc_terms.astype(jnp.bfloat16), 'head').astype(jnp.float32)  66.1 us
    psum x1, waiting for transfers between devices, per_device(): lax.psum(proc_terms.astype(jnp.bfloat16), 'head').astype(jnp.float32)  53.4 us
    all_to_all x3, starting transfers between devices, copy_for_each(): lax.all_to_all(jnp.broadcast_to(array[None], (size, *array.shape)), axis,...  31.6 us
    all_to_all x1, waiting for transfers between devices, summed_on_arrival(): blocks = lax.all_to_all(split_up(array, dim, size), axis, 0, 0, tiled=True)  29.2 us
    all_to_all x3, blocking collectives, all_blocks(): parts = lax.all_to_all(parts, axes[k], split_axis=0, concat_axis=0)  25 us
    another operation x2, loops' own time, listed_attend(): result = lax.map(one_block, jnp.arange(rows // BLOCK, dtype=jnp.int32))  20.2 us
  transfers between devices with their start and end apart: 24, of which 12 were waited for; matrix products, arithmetic and copies ran while one was open for 21% of the time, Pallas kernels for 0%

profile of v1, /device:TPU:65, one launch (start us, length us, event | category | flops | bytes accessed | tf_op | source)
XLA Modules:
  0.0 660.6 jit_solution(7989126209290259015)
XLA Ops:
  6.6 1.7 stack.59
  8.2 44.2 %all-to-all-start.2 = ((bf16[16,1,3,32,128]{4,3,2,1,0:T(8,128)(2,1)}), bf16[16,1,3,32,128]{4,3,2,1,0:T(8,128)(2,1)S(1)}, u32[]{:S(2)}, u32[]{:S(2)}) async-start(bf16[16,1,3,32,128]{4,3,2,1,0:T(8,128)(2,1)} %stack.59), calls=%async_computation.2 | async-start | bytes 786432 | tf_op jit(solution)/shard_map/all_to_all | solution.py:28
  54.1 16.2 %all-to-all-done.2 = bf16[16,1,3,32,128]{4,3,2,1,0:T(8,128)(2,1)S(1)} async-done(((bf16[16,1,3,32,128]{4,3,2,1,0:T(8,128)(2,1)}), bf16[16,1,3,32,128]{4,3,2,1,0:T(8,128)(2,1)S(1)}, u32[]{:S(2)}, u32[]{:S(2)}) %all-to-all-start.2) | async-done | bytes 393248 | tf_op jit(solution)/shard_map/all_to_all | solution.py:28
  70.4 10.5 %all_to_all.70 = bf16[2,16,3,32,128]{4,3,2,1,0:T(8,128)(2,1)S(1)} all-to-all(bf16[2,16,3,32,128]{4,3,2,1,0:T(8,128)(2,1)S(1)} %pad_maximum_fusion.5), channel_id=1, replica_groups=mesh['members'=2,'band_0'=16,'band_1'=2,'head'=8] {'band_1'}, dimensions={0} | all-to-all | bytes 1572864 | tf_op jit(solution)/shard_map/all_to_all | solution.py:28
  81.7 6.7 %all-to-all-start.4 = ((bf16[32,128,32]{1,2,0:T(8,128)(2,1)}), bf16[32,128,32]{1,2,0:T(8,128)(2,1)S(1)}, u32[]{:S(2)}, u32[]{:S(2)}) async-start(bf16[32,128,32]{1,2,0:T(8,128)(2,1)} %broadcast_in_dim.140), calls=%async_computation.4 | async-start | bytes 524288 | tf_op jit(solution)/shard_map/all_to_all | solution.py:55
  89.6 2.6 collective-permute-start.1
  92.2 3.0 collective-permute-start
  97.1 7.8 %collective-permute-done.1 = bf16[2,512,128]{2,1,0:T(8,128)(2,1)S(1)} collective-permute-done((bf16[2,512,128]{2,1,0:T(8,128)(2,1)S(1)}, bf16[2,512,128]{2,1,0:T(8,128)(2,1)S(1)}, u32[]{:S(2)}, u32[]{:S(2)}) %collective-permute-start.1) | collective-permute-done | bytes 262176 | tf_op jit(solution)/shard_map/ppermute | solution.py:48
  105.1 5.3 all-to-all-done.4
  111.3 5.3 all-to-all-start.5
  117.2 38.0 %while.34 = (s32[]{:T(128)}, f32[4,128,128]{2,1,0:T(8,128)}, f32[4,128,2]{1,2,0:T(2,128)}, s32[4]{0:T(128)}, s32[4,8]{1,0:T(4,128)S(1)}, /*index=5*/s32[]{:T(128...) while((s32[]{:T(128)}, f32[4,128,128]{2,1,0:T(8,128)}, ...), condition=%wide.region_9.10_spmd, body=%wide.region_4.9_spmd.sunk | while | flops 69223264 | bytes 5784073 | solution.py:181
  157.2 1.4 convolution_convert_fusion.6
  159.9 4.7 all_to_all.71
  165.3 12.5 %all-to-all-start.7 = ((bf16[32,128,32]{1,2,0:T(8,128)(2,1)}), bf16[32,128,32]{1,2,0:T(8,128)(2,1)S(1)}, u32[]{:S(2)}, u32[]{:S(2)}) async-start(bf16[32,128,32]{1,2,0:T(8,128)(2,1)} %broadcast_in_dim.141), calls=%async_computation.7 | async-start | bytes 524288 | tf_op jit(solution)/shard_map/all_to_all | solution.py:55
  178.7 66.1 %all-reduce.5.cloned.1.call-done = bf16[512,1024]{1,0:T(8,128)(2,1)} async-done(((bf16[512,1024]{1,0:T(8,128)(2,1)}), bf16[512,1024]{1,0:T(8,128)(2,1)}) %all-reduce.5.cloned.1.call-update) | async-done | bytes 1048592 | tf_op jit(solution)/shard_map/psum | solution.py:235
  244.9 1.7 fusion.66
  247.9 13.1 %all-to-all-start.10 = ((bf16[16,1,512,32]{2,3,1,0:T(8,128)(2,1)}), bf16[16,1,512,32]{2,3,1,0:T(8,128)(2,1)}, u32[]{:S(2)}, u32[]{:S(2)}) async-start(bf16[16,1,512,32]{2,3,1,0:T(8,128)(2,1)} %stack.71), calls=%async_computation.10 | async-start | bytes 1048576 | tf_op jit(solution)/shard_map/all_to_all | solution.py:28
  262.9 10.5 %collective-permute-start.2 = (bf16[2,512,128]{2,1,0:T(8,128)(2,1)S(1)}, bf16[2,512,128]{2,1,0:T(8,128)(2,1)}, u32[]{:S(2)}, u32[]{:S(2)}) collective-permute-start(bf16[2,512,128]{2,1,0:T(8,128)(2,1)S(1)} %pad_maximum_fusion.10), channel_id=1, source_target_pairs={{0,24},{8,32},{16,40},{24,48},{32,56},{40,64},{48,72},{56,80},{64,... | collective-permute-start | bytes 786440 | tf_op jit(solution)/shard_map/ppermute | solution.py:67
  273.5 2.4 collective-permute-start.3
  276.0 2.1 collective-permute-start.4
  278.1 2.4 collective-permute-start.5
  283.0 3.8 collective-permute-done.2
  288.1 1.7 constant_dynamic-update-slice_fusion.9
  289.8 3.8 collective-permute-done.3
  294.3 3.9 collective-permute-done.4
  301.1 6.6 collective-permute-done.7
  309.3 11.7 %all-to-all-start.8 = ((bf16[16,1,32,512]{3,2,1,0:T(8,128)(2,1)}), bf16[16,1,32,512]{3,2,1,0:T(8,128)(2,1)S(1)}, u32[]{:S(2)}, u32[]{:S(2)}) async-start(bf16[16,1,32,512]{3,2,1,0:T(8,128)(2,1)} %stack.69), calls=%async_computation.8 | async-start | bytes 1048576 | tf_op jit(solution)/shard_map/all_to_all | solution.py:28
  321.7 54.7 %while.35 = (s32[]{:T(128)}, bf16[4,128,128]{2,1,0:T(8,128)(2,1)}, s32[4]{0:T(128)S(1)}, s32[]{:T(128)}, s32[16384]{0:T(1024)S(1)}, /*index=5*/s32[]{:T(128)}, s...) while((s32[]{:T(128)}, bf16[4,128,128]{2,1,0:T(8,128)(2,1)}, ...), condition=%wide.region_19.20_spmd, body=%wide.region_13.19_spmd.sunk | while | flops 211287568 | bytes 26145704 | solution.py:273
  321.7 1.6 fusion.224
  325.2 1.3 convert_reduce_fusion.5
  327.1 1.6 dynamic-slice_bitcast_fusion.3
  328.9 1.8 fusion.225
  335.4 1.6 fusion.224
  338.9 1.3 convert_reduce_fusion.5
  340.8 1.6 dynamic-slice_bitcast_fusion.3
  342.5 1.8 fusion.225
  349.1 1.6 fusion.224
  352.5 1.3 convert_reduce_fusion.5
  354.5 1.6 dynamic-slice_bitcast_fusion.3
  356.2 1.8 fusion.225
  362.7 1.6 fusion.224
  366.2 1.3 convert_reduce_fusion.5
  368.1 1.6 dynamic-slice_bitcast_fusion.3
  369.8 1.8 fusion.225
  376.4 2.4 convolution_convert_fusion.5
  378.9 2.3 pad_maximum_fusion.3
  382.0 3.6 all-to-all-start.11
  385.6 2.3 pad_maximum_fusion.2
  387.9 3.7 all-to-all-start.9
  394.2 11.5 %all-to-all-start = ((bf16[16,1,3,32,128]{4,3,2,1,0:T(8,128)(2,1)}), bf16[16,1,3,32,128]{4,3,2,1,0:T(8,128)(2,1)S(1)}, u32[]{:S(2)}, u32[]{:S(2)}) async-start(bf16[16,1,3,32,128]{4,3,2,1,0:T(8,128)(2,1)} %stack.57), calls=%async_computation | async-start | bytes 786432 | tf_op jit(solution)/shard_map/all_to_all | solution.py:28
  406.8 53.4 %all-reduce.7.cloned.1.call-done = bf16[512,1024]{1,0:T(8,128)(2,1)} async-done(((bf16[512,1024]{1,0:T(8,128)(2,1)}), bf16[512,1024]{1,0:T(8,128)(2,1)}) %all-reduce.7.cloned.1.call-update) | async-done | bytes 1048592 | tf_op jit(solution)/shard_map/psum | solution.py:277
  460.2 2.0 fusion.150
  463.4 5.6 convolution_convert_fusion.7
  469.2 9.8 %all_to_all.72 = bf16[2,16,3,32,128]{4,3,2,1,0:T(8,128)(2,1)S(1)} all-to-all(bf16[2,16,3,32,128]{4,3,2,1,0:T(8,128)(2,1)S(1)} %pad_maximum_fusion.4), channel_id=1, replica_groups=mesh['members'=2,'band_0'=16,'band_1'=2,'head'=8] {'band_1'}, dimensions={0} | all-to-all | bytes 1572864 | tf_op jit(solution)/shard_map/all_to_all | solution.py:28
  480.0 77.1 %all-reduce.9.cloned.1.call-done = bf16[512,1024]{1,0:T(8,128)(2,1)} async-done(((bf16[512,1024]{1,0:T(8,128)(2,1)}), bf16[512,1024]{1,0:T(8,128)(2,1)}) %all-reduce.9.cloned.1.call-update) | async-done | bytes 1048592 | tf_op jit(solution)/shard_map/psum | solution.py:286
  557.0 1.6 fusion.89
  561.0 7.6 %collective-permute-start.9 = (bf16[2,512,128]{2,1,0:T(8,128)(2,1)S(1)}, bf16[2,512,128]{2,1,0:T(8,128)(2,1)S(1)}, u32[]{:S(2)}, u32[]{:S(2)}) collective-permute-start(bf16[2,512,128]{2,1,0:T(8,128)(2,1)S(1)} %pad_maximum_fusion.11), channel_id=1, source_target_pairs={{8,0},{16,8},{24,16},{32,24},{40,32},{48,40},{56,48},{64,56},{72,6... | collective-permute-start | bytes 786440 | tf_op jit(solution)/shard_map/ppermute | solution.py:48
  568.6 3.2 collective-permute-start.8
  572.5 12.4 %all-to-all-start.12 = ((bf16[32,128,32]{1,2,0:T(8,128)(2,1)}), bf16[32,128,32]{1,2,0:T(8,128)(2,1)S(1)}, u32[]{:S(2)}, u32[]{:S(2)}) async-start(bf16[32,128,32]{1,2,0:T(8,128)(2,1)} %broadcast_in_dim.142), calls=%async_computation.12 | async-start | bytes 524288 | tf_op jit(solution)/shard_map/all_to_all | solution.py:55
  585.7 31.9 %while.36 = (s32[]{:T(128)}, bf16[4,128,128]{2,1,0:T(8,128)(2,1)S(1)}, s32[4]{0:T(128)S(1)}, s32[4,8]{1,0:T(4,128)S(1)}, s32[]{:T(128)}, /*index=5*/s32[4]{0:T(1...) while((s32[]{:T(128)}, ...), condition=%wide.region_31.32_spmd, body=%wide.region_26.31_spmd.sunk | while | flops 69812832 | bytes 5553661 | solution.py:181
  617.7 1.4 convolution_convert_fusion.4
  619.1 3.9 all-to-all-start.13
  623.1 29.2 %all-to-all-done.13 = bf16[8,64,1024]{2,1,0:T(8,128)(2,1)S(1)} async-done(((bf16[8,64,1024]{2,1,0:T(8,128)(2,1)}), bf16[8,64,1024]{2,1,0:T(8,128)(2,1)S(1)}, u32[]{:S(2)}, u32[]{:S(2)}) %all-to-all-start.13) | async-done | bytes 1048608 | tf_op jit(solution)/shard_map/all_to_all | solution.py:78
  652.4 1.6 add_convert_fusion
  (347 shorter events, 109.6 us)
Async XLA Ops:
  6.5 45.9 %copy-start.6 = (bf16[512,1024]{1,0:T(8,128)(2,1)S(1)}, bf16[512,1024]{1,0:T(8,128)(2,1)}, u32[]{:S(2)}) copy-start(bf16[512,1024]{1,0:T(8,128)(2,1)} %param.21) | copy-start | bytes 3145732
  6.5 46.2 %copy-start = (bf16[512,1024]{1,0:T(8,128)(2,1)S(1)}, bf16[512,1024]{1,0:T(8,128)(2,1)}, u32[]{:S(2)}) copy-start(bf16[512,1024]{1,0:T(8,128)(2,1)} %param.22) | copy-start | bytes 3145732
  8.2 62.1 %all-to-all-start.2 = ((bf16[16,1,3,32,128]{4,3,2,1,0:T(8,128)(2,1)}), bf16[16,1,3,32,128]{4,3,2,1,0:T(8,128)(2,1)S(1)}, u32[]{:S(2)}, u32[]{:S(2)}) async-start(bf16[16,1,3,32,128]{4,3,2,1,0:T(8,128)(2,1)} %stack.59), calls=%async_computation.2 | async-start | bytes 786432 | tf_op jit(solution)/shard_map/all_to_all | solution.py:28
  54.1 35.0 %copy-start.4 = (bf16[512,1024]{1,0:T(8,128)(2,1)}, bf16[512,1024]{1,0:T(8,128)(2,1)S(1)}, u32[]{:S(2)}) copy-start(bf16[512,1024]{1,0:T(8,128)(2,1)S(1)} %fusion.65) | copy-start | bytes 3145732
  54.1 26.9 %copy-start.23 = (bf16[128,32]{0,1:T(8,128)(2,1)S(1)}, bf16[128,32]{0,1:T(8,128)(2,1)}, u32[]{:S(2)}) copy-start(bf16[128,32]{0,1:T(8,128)(2,1)} %param.24) | copy-start | bytes 24580
  81.7 28.7 %all-to-all-start.4 = ((bf16[32,128,32]{1,2,0:T(8,128)(2,1)}), bf16[32,128,32]{1,2,0:T(8,128)(2,1)S(1)}, u32[]{:S(2)}, u32[]{:S(2)}) async-start(bf16[32,128,32]{1,2,0:T(8,128)(2,1)} %broadcast_in_dim.140), calls=%async_computation.4 | async-start | bytes 524288 | tf_op jit(solution)/shard_map/all_to_all | solution.py:55
  88.6 6.6 %copy-start.26 = (s32[128,8]{0,1:T(8,128)S(1)}, s32[128,8]{0,1:T(8,128)}, u32[]{:S(2)}) copy-start(s32[128,8]{0,1:T(8,128)} %param.31) | copy-start | bytes 12292
  88.6 6.6 %copy-start.27 = (s32[128,8]{0,1:T(8,128)S(1)}, s32[128,8]{0,1:T(8,128)}, u32[]{:S(2)}) copy-start(s32[128,8]{0,1:T(8,128)} %param.33) | copy-start | bytes 12292
  88.7 7.4 %copy-start.28 = (s32[128]{0:T(128)S(1)}, s32[128]{0:T(128)}, u32[]{:S(2)}) copy-start(s32[128]{0:T(128)} %param.32) | copy-start | bytes 1540
  89.6 15.4 %collective-permute-start.1 = (bf16[2,512,128]{2,1,0:T(8,128)(2,1)S(1)}, bf16[2,512,128]{2,1,0:T(8,128)(2,1)S(1)}, u32[]{:S(2)}, u32[]{:S(2)}) collective-permute-start(bf16[2,512,128]{2,1,0:T(8,128)(2,1)S(1)} %pad_maximum_fusion.9), channel_id=1, source_target_pairs={{8,0},{16,8},{24,16},{32,24},{40,32},{48,40},{56,48},{64,56},{72,6... | collective-permute-start | bytes 786440 | tf_op jit(solution)/shard_map/ppermute | solution.py:48
  92.2 12.7 %collective-permute-start = (bf16[2,512,128]{2,1,0:T(8,128)(2,1)S(1)}, bf16[2,512,128]{2,1,0:T(8,128)(2,1)S(1)}, u32[]{:S(2)}, u32[]{:S(2)}) collective-permute-start(bf16[2,512,128]{2,1,0:T(8,128)(2,1)S(1)} %pad_maximum_fusion.9), channel_id=1, source_target_pairs={{0,8},{8,16},{16,24},{24,32},{32,40},{40,48},{48,56},{56,64},{64,7... | collective-permute-start | bytes 786440 | tf_op jit(solution)/shard_map/ppermute | solution.py:45
  97.1 13.3 %copy-start.20 = (bf16[3,32,128]{2,1,0:T(8,128)(2,1)S(1)}, bf16[3,32,128]{2,1,0:T(8,128)(2,1)}, u32[]{:S(2)}) copy-start(bf16[3,32,128]{2,1,0:T(8,128)(2,1)} %param.25) | copy-start | bytes 73732
  110.4 6.7 %copy-start.12 = (bf16[32,128,32]{1,2,0:T(8,128)(2,1)}, bf16[32,128,32]{1,2,0:T(8,128)(2,1)S(1)}, u32[]{:S(2)}) copy-start(bf16[32,128,32]{1,2,0:T(8,128)(2,1)S(1)} %all-to-all-done.4) | copy-start | bytes 786436
  111.3 47.4 %all-to-all-start.5 = ((bf16[16,1,3,32,128]{4,3,2,1,0:T(8,128)(2,1)}), bf16[16,1,3,32,128]{4,3,2,1,0:T(8,128)(2,1)}, u32[]{:S(2)}, u32[]{:S(2)}) async-start(bf16[16,1,3,32,128]{4,3,2,1,0:T(8,128)(2,1)} %stack.64), calls=%async_computation.5 | async-start | bytes 786432 | tf_op jit(solution)/shard_map/all_to_all | solution.py:28
  116.6 128.3 %all-reduce.5.cloned.1.call-start = ((), (), s32[]{:S(2)}) async-start(), calls=%async_computation.14 | async-start | bytes 2097152 | tf_op jit(solution)/shard_map/psum | solution.py:235
  155.2 2.0 copy-start.13
  158.6 6.0 copy-start.24
  165.3 81.7 %all-to-all-start.7 = ((bf16[32,128,32]{1,2,0:T(8,128)(2,1)}), bf16[32,128,32]{1,2,0:T(8,128)(2,1)S(1)}, u32[]{:S(2)}, u32[]{:S(2)}) async-start(bf16[32,128,32]{1,2,0:T(8,128)(2,1)} %broadcast_in_dim.141), calls=%async_computation.7 | async-start | bytes 524288 | tf_op jit(solution)/shard_map/all_to_all | solution.py:55
  178.7 68.3 %copy-start.18 = (bf16[512,32]{0,1:T(8,128)(2,1)S(1)}, bf16[512,32]{0,1:T(8,128)(2,1)}, u32[]{:S(2)}) copy-start(bf16[512,32]{0,1:T(8,128)(2,1)} %param.28) | copy-start | bytes 98308
  244.9 1.7 copy-start.3
  247.0 0.9 copy-start.11
  247.9 60.5 %all-to-all-start.10 = ((bf16[16,1,512,32]{2,3,1,0:T(8,128)(2,1)}), bf16[16,1,512,32]{2,3,1,0:T(8,128)(2,1)}, u32[]{:S(2)}, u32[]{:S(2)}) async-start(bf16[16,1,512,32]{2,3,1,0:T(8,128)(2,1)} %stack.71), calls=%async_computation.10 | async-start | bytes 1048576 | tf_op jit(solution)/shard_map/all_to_all | solution.py:28
  261.0 1.0 copy-start.15
  261.0 1.4 copy-start.14
  261.4 12.0 %copy-start.8 = (s32[16384]{0:T(1024)S(1)}, s32[16384]{0:T(1024)}, u32[]{:S(2)}) copy-start(s32[16384]{0:T(1024)} %param.35) | copy-start | bytes 196612
  262.9 23.9 %collective-permute-start.2 = (bf16[2,512,128]{2,1,0:T(8,128)(2,1)S(1)}, bf16[2,512,128]{2,1,0:T(8,128)(2,1)}, u32[]{:S(2)}, u32[]{:S(2)}) collective-permute-start(bf16[2,512,128]{2,1,0:T(8,128)(2,1)S(1)} %pad_maximum_fusion.10), channel_id=1, source_target_pairs={{0,24},{8,32},{16,40},{24,48},{32,56},{40,64},{48,72},{56,80},{64,... | collective-permute-start | bytes 786440 | tf_op jit(solution)/shard_map/ppermute | solution.py:67
  273.5 20.1 %collective-permute-start.3 = (bf16[2,512,128]{2,1,0:T(8,128)(2,1)S(1)}, bf16[2,512,128]{2,1,0:T(8,128)(2,1)S(1)}, u32[]{:S(2)}, u32[]{:S(2)}) collective-permute-start(bf16[2,512,128]{2,1,0:T(8,128)(2,1)S(1)} %pad_maximum_fusion.10), channel_id=1, source_target_pairs={{0,16},{8,24},{16,32},{24,40},{32,48},{40,56},{48,64},{56,72},{64,... | collective-permute-start | bytes 786440 | tf_op jit(solution)/shard_map/ppermute | solution.py:67
  276.0 22.2 %collective-permute-start.4 = (bf16[2,512,128]{2,1,0:T(8,128)(2,1)S(1)}, bf16[2,512,128]{2,1,0:T(8,128)(2,1)S(1)}, u32[]{:S(2)}, u32[]{:S(2)}) collective-permute-start(bf16[2,512,128]{2,1,0:T(8,128)(2,1)S(1)} %pad_maximum_fusion.10), channel_id=1, source_target_pairs={{0,8},{8,16},{16,24},{24,32},{32,40},{40,48},{48,56},{56,64},{64,7... | collective-permute-start | bytes 786440 | tf_op jit(solution)/shard_map/ppermute | solution.py:67
  278.1 21.6 %collective-permute-start.5 = (bf16[2,512,128]{2,1,0:T(8,128)(2,1)S(1)}, bf16[2,512,128]{2,1,0:T(8,128)(2,1)S(1)}, u32[]{:S(2)}, u32[]{:S(2)}) collective-permute-start(bf16[2,512,128]{2,1,0:T(8,128)(2,1)S(1)} %pad_maximum_fusion.10), channel_id=1, source_target_pairs={{8,0},{16,8},{24,16},{32,24},{40,32},{48,40},{56,48},{64,56},{72,6... | collective-permute-start | bytes 786440 | tf_op jit(solution)/shard_map/ppermute | solution.py:67
  280.6 19.8 %collective-permute-start.6 = (bf16[2,512,128]{2,1,0:T(8,128)(2,1)S(1)}, bf16[2,512,128]{2,1,0:T(8,128)(2,1)S(1)}, u32[]{:S(2)}, u32[]{:S(2)}) collective-permute-start(bf16[2,512,128]{2,1,0:T(8,128)(2,1)S(1)} %pad_maximum_fusion.10), channel_id=1, source_target_pairs={{16,0},{24,8},{32,16},{40,24},{48,32},{56,40},{64,48},{72,56},{80,... | collective-permute-start | bytes 786440 | tf_op jit(solution)/shard_map/ppermute | solution.py:67
  283.0 25.5 %copy-start.19 = (bf16[32,512]{1,0:T(8,128)(2,1)S(1)}, bf16[32,512]{1,0:T(8,128)(2,1)}, u32[]{:S(2)}) copy-start(bf16[32,512]{1,0:T(8,128)(2,1)} %param.27) | copy-start | bytes 98308
  286.8 20.9 %collective-permute-start.7 = (bf16[2,512,128]{2,1,0:T(8,128)(2,1)S(1)}, bf16[2,512,128]{2,1,0:T(8,128)(2,1)S(1)}, u32[]{:S(2)}, u32[]{:S(2)}) collective-permute-start(bf16[2,512,128]{2,1,0:T(8,128)(2,1)S(1)} %pad_maximum_fusion.10), channel_id=1, source_target_pairs={{24,0},{32,8},{40,16},{48,24},{56,32},{64,40},{72,48},{80,56},{88,... | collective-permute-start | bytes 786440 | tf_op jit(solution)/shard_map/ppermute | solution.py:67
  309.3 71.9 %all-to-all-start.8 = ((bf16[16,1,32,512]{3,2,1,0:T(8,128)(2,1)}), bf16[16,1,32,512]{3,2,1,0:T(8,128)(2,1)S(1)}, u32[]{:S(2)}, u32[]{:S(2)}) async-start(bf16[16,1,32,512]{3,2,1,0:T(8,128)(2,1)} %stack.69), calls=%async_computation.8 | async-start | bytes 1048576 | tf_op jit(solution)/shard_map/all_to_all | solution.py:28
  321.0 139.2 %all-reduce.7.cloned.1.call-start = ((), (), s32[]{:S(2)}) async-start(), calls=%async_computation.15 | async-start | bytes 2097152 | tf_op jit(solution)/shard_map/psum | solution.py:277
  328.7 2.0 copy-start.2
  331.9 1.1 copy-start.1
  342.4 2.0 copy-start.2
  345.6 1.1 copy-start.1
  356.0 2.0 copy-start.2
  359.3 1.1 copy-start.1
  369.7 2.0 copy-start.2
  372.9 1.1 copy-start.1
  381.2 0.8 copy-start.9
  382.0 5.9 all-to-all-start.11
  387.9 5.5 copy-start.21
  387.9 5.5 all-to-all-start.9
  394.2 74.9 %all-to-all-start = ((bf16[16,1,3,32,128]{4,3,2,1,0:T(8,128)(2,1)}), bf16[16,1,3,32,128]{4,3,2,1,0:T(8,128)(2,1)S(1)}, u32[]{:S(2)}, u32[]{:S(2)}) async-start(bf16[16,1,3,32,128]{4,3,2,1,0:T(8,128)(2,1)} %stack.57), calls=%async_computation | async-start | bytes 786432 | tf_op jit(solution)/shard_map/all_to_all | solution.py:28
  405.7 151.4 %all-reduce.9.cloned.1.call-start = ((), (), s32[]{:S(2)}) async-start(), calls=%async_computation.16 | async-start | bytes 2097152 | tf_op jit(solution)/shard_map/psum | solution.py:286
  462.2 1.2 copy-start.10
  557.0 1.6 copy-start.7
  559.1 1.0 copy-start.17
  559.1 1.4 copy-start.16
  559.4 12.3 %copy-start.25 = (bf16[128,32]{0,1:T(8,128)(2,1)S(1)}, bf16[128,32]{0,1:T(8,128)(2,1)}, u32[]{:S(2)}) copy-start(bf16[128,32]{0,1:T(8,128)(2,1)} %param.30) | copy-start | bytes 24580
  560.0 24.9 %copy-start.22 = (s32[4,8]{0,1:T(8,128)S(1)}, s32[4,8]{0,1:T(8,128)}, u32[]{:S(2)}) copy-start(s32[4,8]{0,1:T(8,128)} %get-tuple-element.308) | copy-start | bytes 388
  560.0 25.0 %copy-start.29 = (s32[128]{0:T(128)S(1)}, s32[128]{0:T(128)}, u32[]{:S(2)}) copy-start(s32[128]{0:T(128)} %param.34) | copy-start | bytes 1540
  560.0 25.1 %copy-start.5 = (bf16[512,1024]{1,0:T(8,128)(2,1)S(1)}, bf16[512,1024]{1,0:T(8,128)(2,1)}, u32[]{:S(2)}) copy-start(bf16[512,1024]{1,0:T(8,128)(2,1)} %copy-done.4) | copy-start | bytes 3145732
  561.0 24.6 %collective-permute-start.9 = (bf16[2,512,128]{2,1,0:T(8,128)(2,1)S(1)}, bf16[2,512,128]{2,1,0:T(8,128)(2,1)S(1)}, u32[]{:S(2)}, u32[]{:S(2)}) collective-permute-start(bf16[2,512,128]{2,1,0:T(8,128)(2,1)S(1)} %pad_maximum_fusion.11), channel_id=1, source_target_pairs={{8,0},{16,8},{24,16},{32,24},{40,32},{48,40},{56,48},{64,56},{72,6... | collective-permute-start | bytes 786440 | tf_op jit(solution)/shard_map/ppermute | solution.py:48
  568.6 17.0 %collective-permute-start.8 = (bf16[2,512,128]{2,1,0:T(8,128)(2,1)S(1)}, bf16[2,512,128]{2,1,0:T(8,128)(2,1)S(1)}, u32[]{:S(2)}, u32[]{:S(2)}) collective-permute-start(bf16[2,512,128]{2,1,0:T(8,128)(2,1)S(1)} %pad_maximum_fusion.11), channel_id=1, source_target_pairs={{0,8},{8,16},{16,24},{24,32},{32,40},{40,48},{48,56},{56,64},{64,7... | collective-permute-start | bytes 786440 | tf_op jit(solution)/shard_map/ppermute | solution.py:45
  572.5 45.2 %all-to-all-start.12 = ((bf16[32,128,32]{1,2,0:T(8,128)(2,1)}), bf16[32,128,32]{1,2,0:T(8,128)(2,1)S(1)}, u32[]{:S(2)}, u32[]{:S(2)}) async-start(bf16[32,128,32]{1,2,0:T(8,128)(2,1)} %broadcast_in_dim.142), calls=%async_computation.12 | async-start | bytes 524288 | tf_op jit(solution)/shard_map/all_to_all | solution.py:55
  619.1 33.1 %all-to-all-start.13 = ((bf16[8,64,1024]{2,1,0:T(8,128)(2,1)}), bf16[8,64,1024]{2,1,0:T(8,128)(2,1)S(1)}, u32[]{:S(2)}, u32[]{:S(2)}) async-start(bf16[8,64,1024]{2,1,0:T(8,128)(2,1)} %bitcast.83), calls=%async_computation.13 | async-start | bytes 2097152 | tf_op jit(solution)/shard_map/all_to_all | solution.py:78
Sparse Core Ops, SparseCore 0:
  158.8 85.9 all-reduce.4
  379.0 81.1 all-reduce.6
  469.2 87.7 all-reduce.8
